TPU v7x, 32 devices: a whole 2x2x4 slice. The times are simulated.
32 devices in a mesh: ctx: 16 (over z, x, core), wt: 2 (over y).
Axes of the slice: x: 2, y: 2, z: 4, core: 2. Of those that a mesh axis runs over, the one named last changes fastest.
Arguments:
- patches: bfloat16 [8192, 1280], P('ctx'), may hold values from -6 to 6
- vit_gain: float32 [1280], replicated, may hold values from 0.5 to 1.5
- vit_codes: bfloat16 [1280, 3, 1280], P(None, None, 'wt'), may hold values from -1 to 1
- vit_scales: bfloat16 [2], P('wt'), may hold values from 0.5 to 2
- vit_bias: float32 [3, 1280], P(None, 'wt'), may hold values from -3 to 3
- window_ids: int32 [8192], P('ctx'), may hold values from 63 to 8191, as said below
- merger_codes: bfloat16 [4, 1280, 8192], P(None, 'wt', 'ctx'), may hold values from -0.078125 to 0.078125
- merger_scales: bfloat16 [1, 2, 8192], P(None, 'wt', 'ctx'), may hold values from 0.5 to 2
- merger_bias: float32 [8192], P('wt'), may hold values from -3 to 3
- positions: int32 [2048], P('ctx'), may hold values from 0 to 8191, as said below
- text_embed: bfloat16 [8192, 8192], P('ctx', 'wt'), may hold values from -6 to 6
- norm_gain: float32 [8192], P('wt'), may hold values from 0.5 to 1.5
- llm_codes: bfloat16 [8192, 8, 768], P('wt', None, 'ctx'), may hold values from -1 to 1
- llm_scales: bfloat16 [2, 8, 768], P('wt', None, 'ctx'), may hold values from 0.5 to 2
- llm_bias: float32 [8, 768], P('wt'), may hold values from -3 to 3
- segments: int32 [8192], P('ctx'), may hold values from 0 to 7, never falling along the last dimension, each value on 1 to 2048 neighbouring positions
Outputs:
- attention_out: bfloat16 [8192, 4096], P('ctx', 'wt')
Inputs may be any that keep to these rules, and one draw needn't show every extreme that they name: `window_ids`: windows are runs of consecutive patches of at most 64, never crossing a block of 512 patches; patches of one window share the id, different windows have different ids. `positions`: distinct. The 128 entries of one aligned block (one device's merged tokens) put at most 16 into any one block of 512 positions, and exactly 16 into some block. `segments`: never falling; each run of equal ids is at most 2048 positions long.
All inputs are finite; a program needn't handle non-finite values.
Results may differ from a plain program's by a relative error of at most 0.025.
Values may be sent and summed in bfloat16 or wider, within the bound.
No kernel may reach another device: no remote copies, remote signals or barrier semaphores. Data moves between devices by JAX's collectives and lax.ppermute only.
A program may use at most 192 MiB of HBM per device.

v0:
```python
import jax
import jax.numpy as jnp
from jax import lax
from jax.sharding import PartitionSpec as P

VHD = 80
D = 8192
KVH = 8
HD = 128
GROUP = 4
MERGE = 4
REACH = 4
VIT_EPS = 1e-06
RMS_EPS = 1e-06
ROPE_BASE = 1000000.0
FILL_LOW = -1e30


def passed_along(value, axis, steps):
    count = lax.axis_size(axis)
    leading, last = (max(0, -steps), min(count, count - steps))
    return lax.ppermute(value, axis, [(source, source + steps) for source in range(leading, last)])


def softmax_rows(scores, allowed):
    masked = jnp.where(allowed, scores, FILL_LOW)
    highest = jnp.max(masked, axis=-1, keepdims=True)
    raised = jnp.exp(masked - highest)
    return raised / jnp.sum(raised, axis=-1, keepdims=True)


def vision_norm_rows(patches, vit_gain):
    values = patches.astype(jnp.float32)
    mean_square = jnp.mean(values * values, axis=1, keepdims=True)
    return (values * lax.rsqrt(mean_square + VIT_EPS) * vit_gain).astype(jnp.bfloat16)


def window_attention(normed, weight_block, bias_block, window_ids):
    row_count = normed.shape[0]
    packed = jnp.dot(
        normed, weight_block.reshape(normed.shape[1], -1), preferred_element_type=jnp.float32
    )
    triple = (packed.reshape(row_count, 3, -1) + bias_block).astype(jnp.bfloat16)
    heads_here = triple.shape[2] // VHD
    queries = triple[:, 0].reshape(row_count, heads_here, VHD)
    keys_here = triple[:, 1].reshape(row_count, heads_here, VHD)
    values_here = triple[:, 2].reshape(row_count, heads_here, VHD)
    scores = jnp.einsum(
        "qhd,khd->hqk", queries, keys_here, preferred_element_type=jnp.float32
    ) * VHD ** (-0.5)
    allowed = window_ids[:, None] == window_ids[None, :]
    softmaxed = softmax_rows(scores, allowed[None]).astype(jnp.bfloat16)
    blended = jnp.einsum("hqk,khd->qhd", softmaxed, values_here, preferred_element_type=jnp.float32)
    return blended.astype(jnp.bfloat16).reshape(row_count, -1)


def rope_tables(first, length):
    places = (first + jnp.arange(length, dtype=jnp.int32)).astype(jnp.float32)
    frequency = ROPE_BASE ** (-jnp.arange(0, HD, 2).astype(jnp.float32) / HD)
    angles = places[:, None] * frequency[None, :]
    angles = jnp.concatenate([angles, angles], axis=1)
    return (jnp.cos(angles), jnp.sin(angles))


def rotary(inputs, cosine, sine):
    halfway = inputs.shape[-1] // 2
    turned = jnp.concatenate([-inputs[..., halfway:], inputs[..., :halfway]], axis=-1)
    return inputs * cosine + turned * sine


def split_heads(triple, cosine, sine):
    row_count, group_count = (triple.shape[0], triple.shape[1])
    queries = triple[:, :, : GROUP * HD].reshape(row_count, group_count, GROUP, HD)
    queries = rotary(queries, cosine[:, None, None, :], sine[:, None, None, :]).astype(jnp.bfloat16)
    keys_rot = rotary(
        triple[:, :, GROUP * HD : (GROUP + 1) * HD], cosine[:, None, :], sine[:, None, :]
    ).astype(jnp.bfloat16)
    values_cut = triple[:, :, (GROUP + 1) * HD :].astype(jnp.bfloat16)
    return (queries, keys_rot, values_cut)


def merge_project(features, merger_codes, merger_scales, merger_bias):
    row_count = features.shape[0]
    flat = features.reshape(row_count, -1)
    codes_piece = lax.all_gather(merger_codes, "ctx", axis=2, tiled=True)
    scale_piece = lax.all_gather(merger_scales, "ctx", axis=2, tiled=True)
    width = codes_piece.shape[2]
    dequant = (codes_piece.astype(jnp.float32) * scale_piece.astype(jnp.float32)).astype(
        jnp.bfloat16
    )
    product = jnp.dot(flat, dequant.reshape(-1, width), preferred_element_type=jnp.float32)
    mine = lax.psum_scatter(
        product.astype(jnp.bfloat16), "wt", scatter_dimension=1, tiled=True
    ).astype(jnp.float32)
    return (mine + merger_bias).astype(jnp.bfloat16)


def route_tokens(values, positions, span):
    owners = lax.axis_size("ctx")
    items = values.shape[0]
    capacity = 2 * positions.shape[0] // owners
    target = positions // span
    item_order = jnp.arange(items, dtype=jnp.int32)
    before = (target[None, :] == target[:, None]) & (item_order[None, :] < item_order[:, None])
    ranks = jnp.sum(before.astype(jnp.int32), axis=1)
    slots = target * capacity + ranks
    table = slots[None, :] == jnp.arange(owners * capacity, dtype=jnp.int32)[:, None]
    packed = jnp.dot(table.astype(jnp.bfloat16), values, preferred_element_type=jnp.float32).astype(
        jnp.bfloat16
    )
    labels = jnp.sum(jnp.where(table, positions[None, :] + 1, 0), axis=1) - 1
    return (
        lax.all_to_all(packed, "ctx", split_axis=0, concat_axis=0, tiled=True),
        lax.all_to_all(labels, "ctx", split_axis=0, concat_axis=0, tiled=True),
    )


def place_tokens(text_embed, arrived, labels, first):
    local = labels - first
    table = local[None, :] == jnp.arange(text_embed.shape[0], dtype=jnp.int32)[:, None]
    filled = jnp.dot(
        table.astype(jnp.bfloat16), arrived, preferred_element_type=jnp.float32
    ).astype(jnp.bfloat16)
    covered = jnp.any(table, axis=1)
    return jnp.where(covered[:, None], filled, text_embed)


def on_device(
    patches,
    vit_gain,
    vit_codes,
    vit_scales,
    vit_bias,
    window_ids,
    merger_codes,
    merger_scales,
    merger_bias,
    positions,
    text_embed,
    norm_gain,
    llm_codes,
    llm_scales,
    llm_bias,
    segments,
):
    row_count = text_embed.shape[0]
    first = lax.axis_index("ctx") * row_count
    normed_patches = vision_norm_rows(patches, vit_gain)
    vit_weight = (vit_codes.astype(jnp.float32) * vit_scales.astype(jnp.float32)[0]).astype(
        jnp.bfloat16
    )
    attended = window_attention(normed_patches, vit_weight, vit_bias, window_ids)
    token_count = positions.shape[0]
    features = attended.reshape(token_count, MERGE, -1)
    projected = merge_project(features, merger_codes, merger_scales, merger_bias)
    embedded, labels = route_tokens(projected, positions, row_count)
    hidden = place_tokens(text_embed, embedded, labels, first)
    values = hidden.astype(jnp.float32)
    squares = lax.psum(jnp.sum(values * values, axis=1), "wt")
    normed = (values * lax.rsqrt(squares[:, None] / D + RMS_EPS) * norm_gain).astype(jnp.bfloat16)
    local_rows = normed.shape[1]
    codes_piece = lax.all_gather(llm_codes, "ctx", axis=2, tiled=True)
    scale_piece = lax.all_gather(llm_scales, "ctx", axis=2, tiled=True)
    width = codes_piece.shape[2]
    dequant_piece = (codes_piece.astype(jnp.float32) * scale_piece.astype(jnp.float32)).astype(
        jnp.bfloat16
    )
    product = jnp.dot(
        normed, dequant_piece.reshape(local_rows, -1), preferred_element_type=jnp.float32
    )
    partial_value = product.reshape(row_count, KVH, width)
    triple = (
        lax.psum_scatter(
            partial_value.astype(jnp.bfloat16), "wt", scatter_dimension=1, tiled=True
        ).astype(jnp.float32)
        + llm_bias
    )
    cosine, sine = rope_tables(first, row_count)
    queries, keys_rot, values_cut = split_heads(triple, cosine, sine)
    own = (keys_rot, values_cut, segments)
    arrivals = [own]
    moving = own
    for distance in range(REACH):
        moving = passed_along((moving[0], moving[1], moving[2]), "ctx", 1)
        arrivals.append(moving)
    keys_all = jnp.concatenate([arrival[0] for arrival in arrivals], axis=0)
    values_all = jnp.concatenate([arrival[1] for arrival in arrivals], axis=0)
    key_segments = jnp.concatenate([arrival[2] for arrival in arrivals], axis=0)
    key_places = jnp.concatenate(
        [
            first - distance * row_count + jnp.arange(row_count, dtype=jnp.int32)
            for distance in range(REACH + 1)
        ],
        axis=0,
    )
    query_places = first + jnp.arange(row_count, dtype=jnp.int32)
    allowed = (
        (segments[:, None] == key_segments[None, :])
        & (key_places[None, :] <= query_places[:, None])
        & (key_places[None, :] >= 0)
    )
    outputs = []
    for group_index in range(queries.shape[1]):
        scores = jnp.einsum(
            "qjd,kd->jqk",
            queries[:, group_index],
            keys_all[:, group_index],
            preferred_element_type=jnp.float32,
        ) * HD ** (-0.5)
        softmaxed = softmax_rows(scores, allowed[None]).astype(jnp.bfloat16)
        blended = jnp.einsum(
            "jqk,kd->qjd", softmaxed, values_all[:, group_index], preferred_element_type=jnp.float32
        )
        outputs.append(blended.astype(jnp.bfloat16).reshape(row_count, -1))
    return jnp.concatenate(outputs, axis=1)


def solution(mesh):
    in_specs = (
        P("ctx", None),
        P(),
        P(None, None, "wt"),
        P("wt"),
        P(None, "wt"),
        P("ctx"),
        P(None, "wt", "ctx"),
        P(None, "wt", "ctx"),
        P("wt"),
        P("ctx"),
        P("ctx", "wt"),
        P("wt"),
        P("wt", None, "ctx"),
        P("wt", None, "ctx"),
        P("wt", None),
        P("ctx"),
    )
    out_specs = P("ctx", "wt")
    return jax.shard_map(
        on_device, mesh=mesh, in_specs=in_specs, out_specs=out_specs, check_vma=False
    )
```

profile of v0, /device:TPU:1, one launch (start us, length us, event | category | flops | bytes accessed | tf_op | source)
XLA Modules:
  0.0 852.8 jit_solution(12550410183688036739)
XLA Ops:
  7.3 8.3 copy.82
  16.6 6.4 add_convert_fusion
  24.2 5.5 fusion.104
  29.7 4.3 fusion.75
  34.7 2.1 reshape_reshape_reshape.3
  36.8 23.8 %all_gather.13 = bf16[1,1,8192]{2,1,0:T(2,128)(2,1)S(1)} all-gather(bf16[1,1,512]{2,1,0:T(2,128)(2,1)S(1)} %copy-done.10), channel_id=1, replica_groups=mesh['ctx'=16,'wt'=2] {'ctx'}, dimensions={2}, use_global_device_ids=true | all-gather | bytes 17408 | tf_op jit(solution)/shard_map/all_gather | solution.py:86
  60.6 158.5 %all-gather.3.cloned.1.call-done = bf16[4,640,8192]{2,1,0:T(8,128)(2,1)} async-done(((bf16[4,640,512]{2,1,0:T(8,128)(2,1)}), bf16[4,640,8192]{2,1,0:T(8,128)(2,1)}) %all-gather.3.cloned.1.call-update) | async-done | bytes 41943056 | tf_op jit(solution)/shard_map/all_gather | solution.py:85
  219.1 28.4 %multiply_convert_fusion.1 = bf16[4,640,8192]{2,1,0:T(8,128)(2,1)} fusion(bf16[4,640,8192]{2,1,0:T(8,128)(2,1)} %all-gather.3.cloned.1.call-done, f32[8192]{0:T(1024)S(1)} %bitcast.234), kind=kLoop, calls=%fused_computation.6 | loop fusion | flops 62914560 | bytes 83918848 | tf_op jit(solution)/shard_map/convert_element_type | solution.py:88
  247.4 17.2 %convolution_convert_fusion = bf16[128,8192]{1,0:T(8,128)(2,1)} fusion(bf16[128,2560]{1,0:T(8,128)(2,1)S(1)} %reshape_reshape_reshape.3, bf16[2560,8192]{1,0:T(8,128)(2,1)} %bitcast.224), kind=kOutput, calls=%fused_computation.45 | convolution fusion | flops 5369757696 | bytes 44695552 | tf_op jit(solution)/shard_map/dot_general | solution.py:91
  266.4 5.0 all-to-all-start
  271.4 24.8 %reduce-scatter.3.cloned.1.call-done = bf16[128,4096]{1,0:T(8,128)(2,1)} async-done(((bf16[128,8192]{1,0:T(8,128)(2,1)}), bf16[128,4096]{1,0:T(8,128)(2,1)}) %reduce-scatter.3.cloned.1.call-update) | async-done | bytes 1048592 | tf_op jit(solution)/shard_map/reduce_scatter | solution.py:92
  296.3 3.3 convolution_convert_fusion.2
  299.5 6.4 all-to-all-start.1
  306.1 87.5 %all_gather.15 = bf16[1,8,768]{1,0,2:T(2,128)(2,1)S(1)} all-gather(bf16[1,8,48]{1,0,2:T(2,128)(2,1)S(1)} %copy.88), channel_id=1, replica_groups=mesh['ctx'=16,'wt'=2] {'ctx'}, dimensions={2}, use_global_device_ids=true | all-gather | bytes 13056 | tf_op jit(solution)/shard_map/all_gather | solution.py:163
  394.4 4.9 fusion.29
  399.3 4.2 psum.7
  403.5 177.3 %all-gather.5.cloned.1.call-done = bf16[4096,8,768]{0,2,1:T(8,128)(2,1)} async-done(((bf16[4096,8,48]{0,2,1:T(8,128)(2,1)}), bf16[4096,8,768]{0,2,1:T(8,128)(2,1)}) %all-gather.5.cloned.1.call-update) | async-done | bytes 50331664 | tf_op jit(solution)/shard_map/all_gather | solution.py:162
  580.8 33.5 %fusion.48 = bf16[512,8,768]{2,0,1:T(8,128)(2,1)} fusion(bf16[4096,8,768]{0,2,1:T(8,128)(2,1)} %all-gather.5.cloned.1.call-done, f32[8,768]{1,0:T(8,128)S(1)} %copy.89, bf16[512,4096]{1,0:T(8,128)(2,1)} %get-tuple-element.25, f32[4096]{0:T(1024)S(1)} %copy-done.12, f32[512]{0:T(512)S(1)} %add_rsqrt_fusion), kind=kOutput, calls=%fused_computation.75 | convolution fusion | flops 25856835584 | bytes 60860416 | tf_op jit(solution)/shard_map/dot_general | solution.py:168
  614.9 3.4 collective-permute-start.4
  619.8 3.3 collective-permute-start.5
  623.8 13.5 %collective-permute-start.6 = (s32[512]{0:T(512)S(1)}, s32[512]{0:T(512)S(1)}, u32[]{:S(2)}, u32[]{:S(2)}) collective-permute-start(s32[512]{0:T(512)S(1)} %collective-permute-done.5), channel_id=1, source_target_pairs={{0,2},{2,4},{4,6},{6,8},{8,10},{10,12},{12,14},{14,16},{16,18},{18... | collective-permute-start | bytes 6152 | tf_op jit(solution)/shard_map/ppermute | solution.py:22
  638.0 4.2 collective-permute-start.7
  642.9 58.9 %reduce-scatter.5.cloned.1.call-done = bf16[512,4,768]{2,0,1:T(8,128)(2,1)} async-done(((bf16[512,8,768]{2,0,1:T(8,128)(2,1)}), bf16[512,4,768]{2,0,1:T(8,128)(2,1)}) %reduce-scatter.5.cloned.1.call-update) | async-done | bytes 3145744 | tf_op jit(solution)/shard_map/reduce_scatter | solution.py:173
  701.8 2.4 convert_add_fusion
  704.6 1.6 constant_dynamic-update-slice_fusion.4
  706.2 3.8 collective-permute-start.8
  710.0 1.9 collective-permute-start
  712.0 2.3 and_and_fusion
  716.1 4.4 collective-permute-start.9
  721.8 4.4 collective-permute-start.1
  727.7 4.2 collective-permute-start.10
  733.0 4.5 collective-permute-start.2
  737.5 2.5 fusion.41
  740.9 2.1 collective-permute-start.11
  743.9 1.9 constant_dynamic-update-slice_fusion.9
  745.8 1.9 constant_dynamic-update-slice_fusion.2
  747.8 4.7 collective-permute-start.3
  753.4 2.0 constant_dynamic-update-slice_fusion.1
  756.3 12.6 %fusion.108 = (f32[4,512]{1,0:T(4,128)S(1)}, f32[4,512,2560]{1,2,0:T(8,128)}) fusion(pred[512,2560]{0,1:T(8,128)(4,1)S(1)} %and_and_fusion, bf16[2560,4,128]{2,0,1:T(8,128)(2,1)} %constant_dynamic-update-slice_fusion.7, bf16[512,4,4,128]{3,0,2,1:T(8,128)(2,1)S(1)} %copy-done), kind=kOutput, calls=%fused_computation.183 | convolution fusion | flops 1363151360 | bytes 23470080 | tf_op jit(solution)/shard_map/sub | solution.py:28
  768.9 12.6 %fusion.107 = (f32[4,512]{1,0:T(4,128)S(1)}, f32[4,512,2560]{1,2,0:T(8,128)}) fusion(pred[512,2560]{0,1:T(8,128)(4,1)S(1)} %and_and_fusion, bf16[2560,4,128]{2,0,1:T(8,128)(2,1)} %constant_dynamic-update-slice_fusion.7, bf16[512,4,4,128]{3,0,2,1:T(8,128)(2,1)S(1)} %copy-done), kind=kOutput, calls=%fused_computation.182 | convolution fusion | flops 1363151360 | bytes 23470080 | tf_op jit(solution)/shard_map/sub | solution.py:28
  781.4 12.5 %fusion.106 = (f32[4,512]{1,0:T(4,128)S(1)}, f32[4,512,2560]{1,2,0:T(8,128)}) fusion(pred[512,2560]{0,1:T(8,128)(4,1)S(1)} %and_and_fusion, bf16[2560,4,128]{2,0,1:T(8,128)(2,1)} %constant_dynamic-update-slice_fusion.7, bf16[512,4,4,128]{3,0,2,1:T(8,128)(2,1)S(1)} %copy-done), kind=kOutput, calls=%fused_computation.181 | convolution fusion | flops 1363151360 | bytes 23470080 | tf_op jit(solution)/shard_map/sub | solution.py:28
  794.0 12.7 %fusion.105 = (f32[4,512]{1,0:T(4,128)S(1)}, f32[4,512,2560]{1,2,0:T(8,128)}) fusion(pred[512,2560]{0,1:T(8,128)(4,1)S(1)} %and_and_fusion, bf16[2560,4,128]{2,0,1:T(8,128)(2,1)} %constant_dynamic-update-slice_fusion.7, bf16[512,4,4,128]{3,0,2,1:T(8,128)(2,1)S(1)} %copy-done), kind=kOutput, calls=%fused_computation.180 | convolution fusion | flops 1363151360 | bytes 23470080 | tf_op jit(solution)/shard_map/sub | solution.py:28
  806.6 2.0 constant_dynamic-update-slice_fusion
  808.6 8.7 %fusion.74 = bf16[128,4,512]{2,0,1:T(8,128)(2,1)S(1)} fusion(f32[4,512,2560]{1,2,0:T(8,128)} %get-tuple-element.33, f32[4,512]{1,0:T(4,128)S(1)} %get-tuple-element.32, bf16[2560,4,128]{2,0,1:T(8,128)(2,1)} %constant_dynamic-update-slice_fusion), kind=kOutput, calls=%fused_computation.94 | convolution fusion | flops 1352925184 | bytes 22159360 | tf_op jit(solution)/shard_map/jqk,kd->qjd/dot_general | solution.py:211
  817.6 8.7 %fusion.73 = bf16[128,4,512]{2,0,1:T(8,128)(2,1)S(1)} fusion(f32[4,512,2560]{1,2,0:T(8,128)} %get-tuple-element.31, f32[4,512]{1,0:T(4,128)S(1)} %get-tuple-element.30, bf16[2560,4,128]{2,0,1:T(8,128)(2,1)} %constant_dynamic-update-slice_fusion), kind=kOutput, calls=%fused_computation.93 | convolution fusion | flops 1352925184 | bytes 22159360 | tf_op jit(solution)/shard_map/jqk,kd->qjd/dot_general | solution.py:211
  826.6 8.7 %fusion.72 = bf16[128,4,512]{2,0,1:T(8,128)(2,1)S(1)} fusion(f32[4,512,2560]{1,2,0:T(8,128)} %get-tuple-element.29, f32[4,512]{1,0:T(4,128)S(1)} %get-tuple-element.28, bf16[2560,4,128]{2,0,1:T(8,128)(2,1)} %constant_dynamic-update-slice_fusion), kind=kOutput, calls=%fused_computation.92 | convolution fusion | flops 1352925184 | bytes 22159360 | tf_op jit(solution)/shard_map/jqk,kd->qjd/dot_general | solution.py:211
  835.5 8.7 %fusion.71 = bf16[128,4,512]{2,0,1:T(8,128)(2,1)S(1)} fusion(f32[4,512,2560]{1,2,0:T(8,128)} %get-tuple-element.27, f32[4,512]{1,0:T(4,128)S(1)} %get-tuple-element.26, bf16[2560,4,128]{2,0,1:T(8,128)(2,1)} %constant_dynamic-update-slice_fusion), kind=kOutput, calls=%fused_computation.91 | convolution fusion | flops 1352925184 | bytes 22159360 | tf_op jit(solution)/shard_map/jqk,kd->qjd/dot_general | solution.py:211
  844.5 1.6 pad_maximum_fusion
  (104 shorter events, 20.4 us)
Async XLA Ops:
  6.5 212.5 %all-gather.3.cloned.1.call-start = ((), (), s32[]{:S(2)}) async-start(), calls=%async_computation.4 | async-start | bytes 44564480 | tf_op jit(solution)/shard_map/all_gather | solution.py:85
  7.3 9.0 %copy-start.1 = (bf16[512,1280]{1,0:T(8,128)(2,1)S(1)}, bf16[512,1280]{1,0:T(8,128)(2,1)}, u32[]{:S(2)}) copy-start(bf16[512,1280]{1,0:T(8,128)(2,1)} %param.16) | copy-start | bytes 3932164
  7.3 9.4 %copy-start.13 = (f32[3,640]{1,0:T(4,128)S(1)}, f32[3,640]{1,0:T(4,128)}, u32[]{:S(2)}) copy-start(f32[3,640]{1,0:T(4,128)} %param.20) | copy-start | bytes 23044
  7.3 9.4 %copy-start.14 = (f32[1280]{0:T(1024)S(1)}, f32[1280]{0:T(1024)}, u32[]{:S(2)}) copy-start(f32[1280]{0:T(1024)} %param.17) | copy-start | bytes 15364
  7.3 289.0 %reduce-scatter.3.cloned.1.call-start = ((), (), s32[]{:S(2)}) async-start(), calls=%async_computation.5 | async-start | bytes 3145728 | tf_op jit(solution)/shard_map/reduce_scatter | solution.py:92
  23.0 1.0 copy-start.8
  29.7 7.1 copy-start.10
  264.6 0.8 copy-start.15
  264.6 31.7 %copy-start.6 = (f32[4096]{0:T(1024)S(1)}, f32[4096]{0:T(1024)}, u32[]{:S(2)}) copy-start(f32[4096]{0:T(1024)} %param.24) | copy-start | bytes 49156
  264.6 316.2 %all-gather.5.cloned.1.call-start = ((), (), s32[]{:S(2)}) async-start(), calls=%async_computation.6 | async-start | bytes 53477376 | tf_op jit(solution)/shard_map/all_gather | solution.py:162
  265.4 40.6 %copy-start.11 = (bf16[1,8,48]{2,1,0:T(8,128)(2,1)S(1)}, bf16[1,8,48]{2,1,0:T(8,128)(2,1)}, u32[]{:S(2)}) copy-start(bf16[1,8,48]{2,1,0:T(8,128)(2,1)} %param.29) | copy-start | bytes 2308
  266.4 33.1 %all-to-all-start = ((s32[16,16,1]{1,2,0:T(1,128)}), s32[16,16,1]{1,2,0:T(1,128)S(1)}, u32[]{:S(2)}, u32[]{:S(2)}) async-start(s32[16,16,1]{1,2,0:T(1,128)} %bitcast), calls=%async_computation | async-start | bytes 16384 | tf_op jit(solution)/shard_map/all_to_all | solution.py:114
  299.5 94.9 %all-to-all-start.1 = ((bf16[16,16,4096]{2,1,0:T(8,128)(2,1)}), bf16[16,16,4096]{2,1,0:T(8,128)(2,1)S(1)}, u32[]{:S(2)}, u32[]{:S(2)}) async-start(bf16[16,16,4096]{2,1,0:T(8,128)(2,1)} %bitcast.12), calls=%async_computation.2 | async-start | bytes 4194304 | tf_op jit(solution)/shard_map/all_to_all | solution.py:113
  305.9 395.9 %reduce-scatter.5.cloned.1.call-start = ((), (), s32[]{:S(2)}) async-start(), calls=%async_computation.7 | async-start | bytes 9437184 | tf_op jit(solution)/shard_map/reduce_scatter | solution.py:173
  394.4 186.4 %copy-start.12 = (f32[4096]{0:T(1024)S(1)}, f32[4096]{0:T(1024)}, u32[]{:S(2)}) copy-start(f32[4096]{0:T(1024)} %param.27) | copy-start | bytes 49156
  614.3 0.7 copy-start.9
  614.3 87.5 %copy-start.7 = (f32[4,768]{1,0:T(4,128)S(1)}, f32[4,768]{1,0:T(4,128)}, u32[]{:S(2)}) copy-start(f32[4,768]{1,0:T(4,128)} %param.30) | copy-start | bytes 36868
  614.9 4.8 collective-permute-start.4
  619.8 4.0 collective-permute-start.5
  623.8 14.2 %collective-permute-start.6 = (s32[512]{0:T(512)S(1)}, s32[512]{0:T(512)S(1)}, u32[]{:S(2)}, u32[]{:S(2)}) collective-permute-start(s32[512]{0:T(512)S(1)} %collective-permute-done.5), channel_id=1, source_target_pairs={{0,2},{2,4},{4,6},{6,8},{8,10},{10,12},{12,14},{14,16},{16,18},{18... | collective-permute-start | bytes 6152 | tf_op jit(solution)/shard_map/ppermute | solution.py:22
  638.0 4.9 collective-permute-start.7
  706.2 9.9 %collective-permute-start.8 = (bf16[512,4,128]{2,0,1:T(8,128)(2,1)S(1)}, bf16[512,4,128]{2,0,1:T(8,128)(2,1)S(1)}, u32[]{:S(2)}, u32[]{:S(2)}) collective-permute-start(bf16[512,4,128]{2,0,1:T(8,128)(2,1)S(1)} %get-tuple-element.10), channel_id=1, source_target_pairs={{0,2},{2,4},{4,6},{6,8},{8,10},{10,12},{12,14},{14,16},{16,18},{18... | collective-permute-start | bytes 1572872 | tf_op jit(solution)/shard_map/ppermute | solution.py:22
  710.0 11.7 %collective-permute-start = (bf16[512,4,128]{2,0,1:T(8,128)(2,1)S(1)}, bf16[512,4,128]{2,0,1:T(8,128)(2,1)S(1)}, u32[]{:S(2)}, u32[]{:S(2)}) collective-permute-start(bf16[512,4,128]{2,0,1:T(8,128)(2,1)S(1)} %get-tuple-element.6), channel_id=1, source_target_pairs={{0,2},{2,4},{4,6},{6,8},{8,10},{10,12},{12,14},{14,16},{16,18},{18... | collective-permute-start | bytes 1572872 | tf_op jit(solution)/shard_map/ppermute | solution.py:22
  716.1 11.5 %copy-start.4 = (bf16[512,4,128]{2,0,1:T(8,128)(2,1)}, bf16[512,4,128]{2,0,1:T(8,128)(2,1)S(1)}, u32[]{:S(2)}) copy-start(bf16[512,4,128]{2,0,1:T(8,128)(2,1)S(1)} %collective-permute-done.8) | copy-start | bytes 1572868
  716.1 11.5 %collective-permute-start.9 = (bf16[512,4,128]{2,0,1:T(8,128)(2,1)S(1)}, bf16[512,4,128]{2,0,1:T(8,128)(2,1)}, u32[]{:S(2)}, u32[]{:S(2)}) collective-permute-start(bf16[512,4,128]{2,0,1:T(8,128)(2,1)S(1)} %collective-permute-done.8), channel_id=1, source_target_pairs={{0,2},{2,4},{4,6},{6,8},{8,10},{10,12},{12,14},{14,16},{16,18},{18... | collective-permute-start | bytes 1572872 | tf_op jit(solution)/shard_map/ppermute | solution.py:22
  721.8 5.9 copy-start.2
  721.8 11.2 %collective-permute-start.1 = (bf16[512,4,128]{2,0,1:T(8,128)(2,1)S(1)}, bf16[512,4,128]{2,0,1:T(8,128)(2,1)}, u32[]{:S(2)}, u32[]{:S(2)}) collective-permute-start(bf16[512,4,128]{2,0,1:T(8,128)(2,1)S(1)} %collective-permute-done), channel_id=1, source_target_pairs={{0,2},{2,4},{4,6},{6,8},{8,10},{10,12},{12,14},{14,16},{16,18},{18... | collective-permute-start | bytes 1572872 | tf_op jit(solution)/shard_map/ppermute | solution.py:22
  727.7 13.2 %collective-permute-start.10 = (bf16[512,4,128]{2,0,1:T(8,128)(2,1)}, bf16[512,4,128]{2,0,1:T(8,128)(2,1)S(1)}, u32[]{:S(2)}, u32[]{:S(2)}) collective-permute-start(bf16[512,4,128]{2,0,1:T(8,128)(2,1)} %collective-permute-done.9), channel_id=1, source_target_pairs={{0,2},{2,4},{4,6},{6,8},{8,10},{10,12},{12,14},{14,16},{16,18},{18... | collective-permute-start | bytes 1572872 | tf_op jit(solution)/shard_map/ppermute | solution.py:22
  733.0 14.8 %collective-permute-start.2 = (bf16[512,4,128]{2,0,1:T(8,128)(2,1)}, bf16[512,4,128]{2,0,1:T(8,128)(2,1)}, u32[]{:S(2)}, u32[]{:S(2)}) collective-permute-start(bf16[512,4,128]{2,0,1:T(8,128)(2,1)} %collective-permute-done.1), channel_id=1, source_target_pairs={{0,2},{2,4},{4,6},{6,8},{8,10},{10,12},{12,14},{14,16},{16,18},{18... | collective-permute-start | bytes 1572872 | tf_op jit(solution)/shard_map/ppermute | solution.py:22
  737.5 2.5 copy-start.5
  737.5 5.5 copy-start.3
  740.0 16.3 %copy-start = (bf16[512,4,4,128]{3,0,2,1:T(8,128)(2,1)S(1)}, bf16[512,4,4,128]{3,0,2,1:T(8,128)(2,1)}, u32[]{:S(2)}) copy-start(bf16[512,4,4,128]{3,0,2,1:T(8,128)(2,1)} %fusion.41) | copy-start | bytes 6291460
  740.9 14.5 %collective-permute-start.11 = (bf16[512,4,128]{2,0,1:T(8,128)(2,1)S(1)}, bf16[512,4,128]{2,0,1:T(8,128)(2,1)S(1)}, u32[]{:S(2)}, u32[]{:S(2)}) collective-permute-start(bf16[512,4,128]{2,0,1:T(8,128)(2,1)S(1)} %collective-permute-done.10), channel_id=1, source_target_pairs={{0,2},{2,4},{4,6},{6,8},{8,10},{10,12},{12,14},{14,16},{16,18},{18... | collective-permute-start | bytes 1572872 | tf_op jit(solution)/shard_map/ppermute | solution.py:22
  747.8 58.9 %collective-permute-start.3 = (bf16[512,4,128]{2,0,1:T(8,128)(2,1)}, bf16[512,4,128]{2,0,1:T(8,128)(2,1)}, u32[]{:S(2)}, u32[]{:S(2)}) collective-permute-start(bf16[512,4,128]{2,0,1:T(8,128)(2,1)} %collective-permute-done.2), channel_id=1, source_target_pairs={{0,2},{2,4},{4,6},{6,8},{8,10},{10,12},{12,14},{14,16},{16,18},{18... | collective-permute-start | bytes 1572872 | tf_op jit(solution)/shard_map/ppermute | solution.py:22
Sparse Core Ops, SparseCore 0:
  8.9 210.1 all-gather.2
  264.8 31.4 reduce-scatter.2
  297.8 282.9 all-gather.4
  614.4 87.3 reduce-scatter.4
where the time goes:
time: 861 us; the launch traced here: 853 us
  waiting for transfers between devices  427 us (50%)
  matrix products  160 us (19%)
  blocking collectives  115 us (13%)
  starting transfers between devices  65.9 us (8%)
  other arithmetic  43.4 us (5%)
  local copies, waits for them, and re-layouts  26.5 us (3%)
  between operations  14.6 us (2%)
    all_gather x1, waiting for transfers between devices, on_device(): codes_piece = lax.all_gather(llm_codes, 'ctx', axis=2, tiled=True)  177 us
    all_gather x1, waiting for transfers between devices, merge_project(): codes_piece = lax.all_gather(merger_codes, 'ctx', axis=2, tiled=True)  158 us
    all_gather x1, blocking collectives, on_device(): scale_piece = lax.all_gather(llm_scales, 'ctx', axis=2, tiled=True)  87.5 us
    reduce_scatter x1, waiting for transfers between devices, on_device(): lax.psum_scatter(partial_value.astype(jnp.bfloat16), 'wt', scatter_dimens...  58.9 us
    sub x5, matrix products, softmax_rows(): raised = jnp.exp(masked - highest)  55.8 us
    ppermute x12, starting transfers between devices, passed_along(): lax.ppermute(value, axis, [(source, source + steps) for source in range(l...  54.3 us
    dot_general x4, matrix products, on_device(): jnp.einsum('jqk,kd->qjd', softmaxed, values_all[:, group_index], preferre...  35 us
    dot_general x1, matrix products, on_device(): jnp.dot(normed, dequant_piece.reshape(local_rows, -1), preferred_element_...  33.5 us
  transfers between devices with their start and end apart: 18, of which 10 were waited for; matrix products, arithmetic and copies ran while one was open for 13% of the time, Pallas kernels for 0%

commit v1 on v0

--- a/solution.py
+++ b/solution.py
@@ -82,7 +82,7 @@
 def merge_project(features, merger_codes, merger_scales, merger_bias):
     row_count = features.shape[0]
     flat = features.reshape(row_count, -1)
-    codes_piece = lax.all_gather(merger_codes, "ctx", axis=2, tiled=True)
+    codes_piece = jnp.concatenate(lax.all_gather(merger_codes, axis_name="ctx"), axis=2)
     scale_piece = lax.all_gather(merger_scales, "ctx", axis=2, tiled=True)
     width = codes_piece.shape[2]
     dequant = (codes_piece.astype(jnp.float32) * scale_piece.astype(jnp.float32)).astype(

time: 861 us -> 988 us (1.15)
  other arithmetic: 43.4 us -> 132 us
  local copies, waits for them, and re-layouts: 26.5 us -> 64.4 us
    convert_element_type x1, other arithmetic: 28.4 us -> 76.4 us  [merge_project(): (codes_piece.astype(jnp.float32) * scale_piece.astype(jnp.float32)).astyp...]
    convert_element_type x0 -> x1, other arithmetic: none -> 40.6 us  [merge_project(): codes_piece.astype(jnp.float32) * scale_piece.astype(jnp.float32)]
    unnamed x44 -> x45, local copies, waits for them, and re-layouts: 17.7 us -> 55.6 us
  transfers between devices with their start and end apart: 18 -> 18, of which waited for: 10 -> 10; matrix products, arithmetic and copies ran while one was open for 13% -> 11% of each run, Pallas kernels for 0% -> 0%
where the time goes in v1:
time: 988 us; the launch traced here: 979 us
  waiting for transfers between devices  427 us (43%)
  matrix products  160 us (16%)
  other arithmetic  132 us (13%)
  blocking collectives  115 us (12%)
  starting transfers between devices  65.8 us (7%)
  local copies, waits for them, and re-layouts  64.4 us (7%)
  between operations  14.6 us (1%)
    all_gather x1, waiting for transfers between devices, on_device(): codes_piece = lax.all_gather(llm_codes, 'ctx', axis=2, tiled=True)  177 us
    all_gather x1, waiting for transfers between devices, merge_project(): lax.all_gather(merger_codes, axis_name='ctx')  158 us
    all_gather x1, blocking collectives, on_device(): scale_piece = lax.all_gather(llm_scales, 'ctx', axis=2, tiled=True)  87.5 us
    convert_element_type x1, other arithmetic, merge_project(): (codes_piece.astype(jnp.float32) * scale_piece.astype(jnp.float32)).astyp...  76.4 us
    reduce_scatter x1, waiting for transfers between devices, on_device(): lax.psum_scatter(partial_value.astype(jnp.bfloat16), 'wt', scatter_dimens...  59 us
    sub x5, matrix products, softmax_rows(): raised = jnp.exp(masked - highest)  55.8 us
    unnamed x45, local copies, waits for them, and re-layouts  55.6 us
    ppermute x12, starting transfers between devices, passed_along(): lax.ppermute(value, axis, [(source, source + steps) for source in range(l...  54.3 us
  transfers between devices with their start and end apart: 18, of which 10 were waited for; matrix products, arithmetic and copies ran while one was open for 11% of the time, Pallas kernels for 0%

profile of v1, /device:TPU:1, one launch (start us, length us, event | category | flops | bytes accessed | tf_op | source)
XLA Modules:
  0.0 979.5 jit_solution(10207000894229639316)
XLA Ops:
  7.3 8.3 copy.84
  16.6 6.4 add_convert_fusion
  24.2 5.5 fusion.105
  29.7 4.3 fusion.76
  34.7 2.1 reshape_reshape_reshape.3
  36.8 23.8 %all_gather.17 = bf16[1,1,8192]{2,1,0:T(2,128)(2,1)S(1)} all-gather(bf16[1,1,512]{2,1,0:T(2,128)(2,1)S(1)} %copy-done.10), channel_id=1, replica_groups=mesh['ctx'=16,'wt'=2] {'ctx'}, dimensions={2}, use_global_device_ids=true | all-gather | bytes 17408 | tf_op jit(solution)/shard_map/all_gather | solution.py:86
  60.7 158.4 %all-gather.6.cloned.1.call-done = bf16[64,640,512]{2,1,0:T(8,128)(2,1)} async-done(((bf16[4,640,512]{2,1,0:T(8,128)(2,1)}), bf16[64,640,512]{2,1,0:T(8,128)(2,1)}) %all-gather.6.cloned.1.call-update) | async-done | bytes 41943056 | tf_op jit(solution)/shard_map/all_gather | solution.py:85
  219.1 40.6 %convert.8 = f32[16,4,640,512]{3,2,1,0:T(8,128)} convert(bf16[16,4,640,512]{3,2,1,0:T(8,128)(2,1)} %bitcast.230) | non-fusion elementwise | flops 20971520 | bytes 125829120 | tf_op jit(solution)/shard_map/convert_element_type | solution.py:88
  259.8 76.4 %fusion.5 = bf16[16,4,640,512]{3,0,2,1:T(8,128)(2,1)} fusion(f32[16,4,640,512]{3,2,1,0:T(8,128)} %convert.8, f32[16,512]{1,0:T(8,128)S(1)} %reshape.345), kind=kLoop, calls=%fused_computation.7 | loop fusion | flops 41943040 | bytes 125861888 | tf_op jit(solution)/shard_map/convert_element_type | solution.py:88
  336.2 38.0 %copy.122 = bf16[320,8,16,512]{3,1,2,0:T(8,128)(2,1)} copy(bf16[320,8,16,512]{3,2,1,0:T(8,128)(2,1)} %bitcast.229) | data formatting | bytes 83886080
  374.2 17.2 %convolution_convert_fusion = bf16[128,8192]{1,0:T(8,128)(2,1)} fusion(bf16[128,2560]{1,0:T(8,128)(2,1)S(1)} %reshape_reshape_reshape.3, bf16[2560,8192]{1,0:T(8,128)(2,1)} %bitcast.228), kind=kOutput, calls=%fused_computation.46 | convolution fusion | flops 5369757696 | bytes 44695552 | tf_op jit(solution)/shard_map/dot_general | solution.py:91
  393.2 5.0 all-to-all-start
  398.2 24.8 %reduce-scatter.3.cloned.1.call-done = bf16[128,4096]{1,0:T(8,128)(2,1)} async-done(((bf16[128,8192]{1,0:T(8,128)(2,1)}), bf16[128,4096]{1,0:T(8,128)(2,1)}) %reduce-scatter.3.cloned.1.call-update) | async-done | bytes 1048592 | tf_op jit(solution)/shard_map/reduce_scatter | solution.py:92
  423.0 3.3 convolution_convert_fusion.2
  426.3 6.4 all-to-all-start.1
  432.8 87.5 %all_gather.19 = bf16[1,8,768]{1,0,2:T(2,128)(2,1)S(1)} all-gather(bf16[1,8,48]{1,0,2:T(2,128)(2,1)S(1)} %copy.91), channel_id=1, replica_groups=mesh['ctx'=16,'wt'=2] {'ctx'}, dimensions={2}, use_global_device_ids=true | all-gather | bytes 13056 | tf_op jit(solution)/shard_map/all_gather | solution.py:163
  521.2 4.9 fusion.30
  526.1 4.2 psum.7
  530.2 177.3 %all-gather.4.cloned.1.call-done = bf16[4096,8,768]{0,2,1:T(8,128)(2,1)} async-done(((bf16[4096,8,48]{0,2,1:T(8,128)(2,1)}), bf16[4096,8,768]{0,2,1:T(8,128)(2,1)}) %all-gather.4.cloned.1.call-update) | async-done | bytes 50331664 | tf_op jit(solution)/shard_map/all_gather | solution.py:162
  707.6 33.5 %fusion.49 = bf16[512,8,768]{2,0,1:T(8,128)(2,1)} fusion(bf16[4096,8,768]{0,2,1:T(8,128)(2,1)} %all-gather.4.cloned.1.call-done, f32[8,768]{1,0:T(8,128)S(1)} %copy.92, bf16[512,4096]{1,0:T(8,128)(2,1)} %get-tuple-element.25, f32[4096]{0:T(1024)S(1)} %copy-done.12, f32[512]{0:T(512)S(1)} %add_rsqrt_fusion), kind=kOutput, calls=%fused_computation.76 | convolution fusion | flops 25856835584 | bytes 60860416 | tf_op jit(solution)/shard_map/dot_general | solution.py:168
  741.7 3.2 collective-permute-start.4
  746.4 3.5 collective-permute-start.5
  750.6 13.3 %collective-permute-start.6 = (s32[512]{0:T(512)S(1)}, s32[512]{0:T(512)S(1)}, u32[]{:S(2)}, u32[]{:S(2)}) collective-permute-start(s32[512]{0:T(512)S(1)} %collective-permute-done.5), channel_id=1, source_target_pairs={{0,2},{2,4},{4,6},{6,8},{8,10},{10,12},{12,14},{14,16},{16,18},{18... | collective-permute-start | bytes 6152 | tf_op jit(solution)/shard_map/ppermute | solution.py:22
  764.6 4.4 collective-permute-start.7
  769.6 59.0 %reduce-scatter.5.cloned.1.call-done = bf16[512,4,768]{2,0,1:T(8,128)(2,1)} async-done(((bf16[512,8,768]{2,0,1:T(8,128)(2,1)}), bf16[512,4,768]{2,0,1:T(8,128)(2,1)}) %reduce-scatter.5.cloned.1.call-update) | async-done | bytes 3145744 | tf_op jit(solution)/shard_map/reduce_scatter | solution.py:173
  828.6 2.4 convert_add_fusion
  833.0 3.8 collective-permute-start.8
  836.8 1.9 collective-permute-start
  838.7 2.3 and_and_fusion
  842.9 4.4 collective-permute-start.9
  848.5 4.4 collective-permute-start.1
  854.4 4.2 collective-permute-start.10
  859.8 4.5 collective-permute-start.2
  864.3 2.5 fusion.42
  867.7 2.1 collective-permute-start.11
  870.7 1.9 constant_dynamic-update-slice_fusion.9
  872.6 1.9 constant_dynamic-update-slice_fusion.2
  874.5 4.7 collective-permute-start.3
  880.2 1.9 constant_dynamic-update-slice_fusion.1
  883.0 12.6 %fusion.109 = (f32[4,512]{1,0:T(4,128)S(1)}, f32[4,512,2560]{1,2,0:T(8,128)}) fusion(pred[512,2560]{0,1:T(8,128)(4,1)S(1)} %and_and_fusion, bf16[2560,4,128]{2,0,1:T(8,128)(2,1)} %constant_dynamic-update-slice_fusion.7, bf16[512,4,4,128]{3,0,2,1:T(8,128)(2,1)S(1)} %copy-done), kind=kOutput, calls=%fused_computation.185 | convolution fusion | flops 1363151360 | bytes 23470080 | tf_op jit(solution)/shard_map/sub | solution.py:28
  895.6 12.6 %fusion.108 = (f32[4,512]{1,0:T(4,128)S(1)}, f32[4,512,2560]{1,2,0:T(8,128)}) fusion(pred[512,2560]{0,1:T(8,128)(4,1)S(1)} %and_and_fusion, bf16[2560,4,128]{2,0,1:T(8,128)(2,1)} %constant_dynamic-update-slice_fusion.7, bf16[512,4,4,128]{3,0,2,1:T(8,128)(2,1)S(1)} %copy-done), kind=kOutput, calls=%fused_computation.184 | convolution fusion | flops 1363151360 | bytes 23470080 | tf_op jit(solution)/shard_map/sub | solution.py:28
  908.1 12.5 %fusion.107 = (f32[4,512]{1,0:T(4,128)S(1)}, f32[4,512,2560]{1,2,0:T(8,128)}) fusion(pred[512,2560]{0,1:T(8,128)(4,1)S(1)} %and_and_fusion, bf16[2560,4,128]{2,0,1:T(8,128)(2,1)} %constant_dynamic-update-slice_fusion.7, bf16[512,4,4,128]{3,0,2,1:T(8,128)(2,1)S(1)} %copy-done), kind=kOutput, calls=%fused_computation.183 | convolution fusion | flops 1363151360 | bytes 23470080 | tf_op jit(solution)/shard_map/sub | solution.py:28
  920.7 12.7 %fusion.106 = (f32[4,512]{1,0:T(4,128)S(1)}, f32[4,512,2560]{1,2,0:T(8,128)}) fusion(pred[512,2560]{0,1:T(8,128)(4,1)S(1)} %and_and_fusion, bf16[2560,4,128]{2,0,1:T(8,128)(2,1)} %constant_dynamic-update-slice_fusion.7, bf16[512,4,4,128]{3,0,2,1:T(8,128)(2,1)S(1)} %copy-done), kind=kOutput, calls=%fused_computation.182 | convolution fusion | flops 1363151360 | bytes 23470080 | tf_op jit(solution)/shard_map/sub | solution.py:28
  933.3 1.9 constant_dynamic-update-slice_fusion
  935.3 8.7 fusion.75
  944.2 8.7 fusion.74
  953.2 8.7 fusion.73
  962.2 8.7 fusion.72
  (107 shorter events, 23.6 us)
Async XLA Ops:
  6.5 212.6 %all-gather.6.cloned.1.call-start = ((), (), s32[]{:S(2)}) async-start(), calls=%async_computation.7 | async-start | bytes 44564480 | tf_op jit(solution)/shard_map/all_gather | solution.py:85
  7.3 9.0 copy-start.1
  7.3 9.4 copy-start.13
  7.3 9.4 copy-start.14
  7.3 415.8 %reduce-scatter.3.cloned.1.call-start = ((), (), s32[]{:S(2)}) async-start(), calls=%async_computation.4 | async-start | bytes 3145728 | tf_op jit(solution)/shard_map/reduce_scatter | solution.py:92
  23.0 1.0 copy-start.8
  29.7 7.1 copy-start.10
  391.4 0.8 copy-start.15
  391.4 31.7 %copy-start.6 = (f32[4096]{0:T(1024)S(1)}, f32[4096]{0:T(1024)}, u32[]{:S(2)}) copy-start(f32[4096]{0:T(1024)} %param.24) | copy-start | bytes 49156
  391.4 316.2 %all-gather.4.cloned.1.call-start = ((), (), s32[]{:S(2)}) async-start(), calls=%async_computation.5 | async-start | bytes 53477376 | tf_op jit(solution)/shard_map/all_gather | solution.py:162
  392.1 40.6 %copy-start.11 = (bf16[1,8,48]{2,1,0:T(8,128)(2,1)S(1)}, bf16[1,8,48]{2,1,0:T(8,128)(2,1)}, u32[]{:S(2)}) copy-start(bf16[1,8,48]{2,1,0:T(8,128)(2,1)} %param.29) | copy-start | bytes 2308
  393.2 33.1 %all-to-all-start = ((s32[16,16,1]{1,2,0:T(1,128)}), s32[16,16,1]{1,2,0:T(1,128)S(1)}, u32[]{:S(2)}, u32[]{:S(2)}) async-start(s32[16,16,1]{1,2,0:T(1,128)} %bitcast), calls=%async_computation | async-start | bytes 16384 | tf_op jit(solution)/shard_map/all_to_all | solution.py:114
  426.3 94.9 %all-to-all-start.1 = ((bf16[16,16,4096]{2,1,0:T(8,128)(2,1)}), bf16[16,16,4096]{2,1,0:T(8,128)(2,1)S(1)}, u32[]{:S(2)}, u32[]{:S(2)}) async-start(bf16[16,16,4096]{2,1,0:T(8,128)(2,1)} %bitcast.12), calls=%async_computation.2 | async-start | bytes 4194304 | tf_op jit(solution)/shard_map/all_to_all | solution.py:113
  432.7 395.9 %reduce-scatter.5.cloned.1.call-start = ((), (), s32[]{:S(2)}) async-start(), calls=%async_computation.6 | async-start | bytes 9437184 | tf_op jit(solution)/shard_map/reduce_scatter | solution.py:173
  521.2 186.4 %copy-start.12 = (f32[4096]{0:T(1024)S(1)}, f32[4096]{0:T(1024)}, u32[]{:S(2)}) copy-start(f32[4096]{0:T(1024)} %param.27) | copy-start | bytes 49156
  741.1 0.7 copy-start.9
  741.1 87.5 %copy-start.7 = (f32[4,768]{1,0:T(4,128)S(1)}, f32[4,768]{1,0:T(4,128)}, u32[]{:S(2)}) copy-start(f32[4,768]{1,0:T(4,128)} %param.30) | copy-start | bytes 36868
  741.7 4.6 collective-permute-start.4
  746.4 4.2 collective-permute-start.5
  750.6 14.0 %collective-permute-start.6 = (s32[512]{0:T(512)S(1)}, s32[512]{0:T(512)S(1)}, u32[]{:S(2)}, u32[]{:S(2)}) collective-permute-start(s32[512]{0:T(512)S(1)} %collective-permute-done.5), channel_id=1, source_target_pairs={{0,2},{2,4},{4,6},{6,8},{8,10},{10,12},{12,14},{14,16},{16,18},{18... | collective-permute-start | bytes 6152 | tf_op jit(solution)/shard_map/ppermute | solution.py:22
  764.6 5.1 collective-permute-start.7
  833.0 9.9 %collective-permute-start.8 = (bf16[512,4,128]{2,0,1:T(8,128)(2,1)S(1)}, bf16[512,4,128]{2,0,1:T(8,128)(2,1)S(1)}, u32[]{:S(2)}, u32[]{:S(2)}) collective-permute-start(bf16[512,4,128]{2,0,1:T(8,128)(2,1)S(1)} %get-tuple-element.10), channel_id=1, source_target_pairs={{0,2},{2,4},{4,6},{6,8},{8,10},{10,12},{12,14},{14,16},{16,18},{18... | collective-permute-start | bytes 1572872 | tf_op jit(solution)/shard_map/ppermute | solution.py:22
  836.8 11.7 %collective-permute-start = (bf16[512,4,128]{2,0,1:T(8,128)(2,1)S(1)}, bf16[512,4,128]{2,0,1:T(8,128)(2,1)S(1)}, u32[]{:S(2)}, u32[]{:S(2)}) collective-permute-start(bf16[512,4,128]{2,0,1:T(8,128)(2,1)S(1)} %get-tuple-element.6), channel_id=1, source_target_pairs={{0,2},{2,4},{4,6},{6,8},{8,10},{10,12},{12,14},{14,16},{16,18},{18... | collective-permute-start | bytes 1572872 | tf_op jit(solution)/shard_map/ppermute | solution.py:22
  842.9 11.5 %copy-start.4 = (bf16[512,4,128]{2,0,1:T(8,128)(2,1)}, bf16[512,4,128]{2,0,1:T(8,128)(2,1)S(1)}, u32[]{:S(2)}) copy-start(bf16[512,4,128]{2,0,1:T(8,128)(2,1)S(1)} %collective-permute-done.8) | copy-start | bytes 1572868
  842.9 11.5 %collective-permute-start.9 = (bf16[512,4,128]{2,0,1:T(8,128)(2,1)S(1)}, bf16[512,4,128]{2,0,1:T(8,128)(2,1)}, u32[]{:S(2)}, u32[]{:S(2)}) collective-permute-start(bf16[512,4,128]{2,0,1:T(8,128)(2,1)S(1)} %collective-permute-done.8), channel_id=1, source_target_pairs={{0,2},{2,4},{4,6},{6,8},{8,10},{10,12},{12,14},{14,16},{16,18},{18... | collective-permute-start | bytes 1572872 | tf_op jit(solution)/shard_map/ppermute | solution.py:22
  848.5 5.9 copy-start.2
  848.5 11.2 %collective-permute-start.1 = (bf16[512,4,128]{2,0,1:T(8,128)(2,1)S(1)}, bf16[512,4,128]{2,0,1:T(8,128)(2,1)}, u32[]{:S(2)}, u32[]{:S(2)}) collective-permute-start(bf16[512,4,128]{2,0,1:T(8,128)(2,1)S(1)} %collective-permute-done), channel_id=1, source_target_pairs={{0,2},{2,4},{4,6},{6,8},{8,10},{10,12},{12,14},{14,16},{16,18},{18... | collective-permute-start | bytes 1572872 | tf_op jit(solution)/shard_map/ppermute | solution.py:22
  854.4 13.2 %collective-permute-start.10 = (bf16[512,4,128]{2,0,1:T(8,128)(2,1)}, bf16[512,4,128]{2,0,1:T(8,128)(2,1)S(1)}, u32[]{:S(2)}, u32[]{:S(2)}) collective-permute-start(bf16[512,4,128]{2,0,1:T(8,128)(2,1)} %collective-permute-done.9), channel_id=1, source_target_pairs={{0,2},{2,4},{4,6},{6,8},{8,10},{10,12},{12,14},{14,16},{16,18},{18... | collective-permute-start | bytes 1572872 | tf_op jit(solution)/shard_map/ppermute | solution.py:22
  859.8 14.8 %collective-permute-start.2 = (bf16[512,4,128]{2,0,1:T(8,128)(2,1)}, bf16[512,4,128]{2,0,1:T(8,128)(2,1)}, u32[]{:S(2)}, u32[]{:S(2)}) collective-permute-start(bf16[512,4,128]{2,0,1:T(8,128)(2,1)} %collective-permute-done.1), channel_id=1, source_target_pairs={{0,2},{2,4},{4,6},{6,8},{8,10},{10,12},{12,14},{14,16},{16,18},{18... | collective-permute-start | bytes 1572872 | tf_op jit(solution)/shard_map/ppermute | solution.py:22
  864.3 2.5 copy-start.5
  864.3 5.5 copy-start.3
  866.7 16.3 %copy-start = (bf16[512,4,4,128]{3,0,2,1:T(8,128)(2,1)S(1)}, bf16[512,4,4,128]{3,0,2,1:T(8,128)(2,1)}, u32[]{:S(2)}) copy-start(bf16[512,4,4,128]{3,0,2,1:T(8,128)(2,1)} %fusion.42) | copy-start | bytes 6291460
  867.7 14.5 %collective-permute-start.11 = (bf16[512,4,128]{2,0,1:T(8,128)(2,1)S(1)}, bf16[512,4,128]{2,0,1:T(8,128)(2,1)S(1)}, u32[]{:S(2)}, u32[]{:S(2)}) collective-permute-start(bf16[512,4,128]{2,0,1:T(8,128)(2,1)S(1)} %collective-permute-done.10), channel_id=1, source_target_pairs={{0,2},{2,4},{4,6},{6,8},{8,10},{10,12},{12,14},{14,16},{16,18},{18... | collective-permute-start | bytes 1572872 | tf_op jit(solution)/shard_map/ppermute | solution.py:22
  874.5 58.8 %collective-permute-start.3 = (bf16[512,4,128]{2,0,1:T(8,128)(2,1)}, bf16[512,4,128]{2,0,1:T(8,128)(2,1)}, u32[]{:S(2)}, u32[]{:S(2)}) collective-permute-start(bf16[512,4,128]{2,0,1:T(8,128)(2,1)} %collective-permute-done.2), channel_id=1, source_target_pairs={{0,2},{2,4},{4,6},{6,8},{8,10},{10,12},{12,14},{14,16},{16,18},{18... | collective-permute-start | bytes 1572872 | tf_op jit(solution)/shard_map/ppermute | solution.py:22
Sparse Core Ops, SparseCore 0:
  8.9 210.1 all-gather.5
  391.5 31.4 reduce-scatter.2
  424.6 282.9 all-gather.3
  741.2 87.3 reduce-scatter.4
